TPU v7x, 512 devices: a 4x2x32 block of a 4x8x32 slice. The times are simulated.
512 devices in a mesh: parts: 2 (over y), seq: 32 (over z), tp: 8 (over x, core).
Axes of the slice: x: 4, y: 2, z: 32, core: 2. Of those that a mesh axis runs over, the one named last changes fastest.
The devices are a block of a 4x8x32 slice.
Arguments:
- tokens: bfloat16 [16384, 8192], P(('parts', 'seq'), 'tp'), parts along dimension 0, may hold values from -6 to 6
- norm_gain: bfloat16 [8192], P('tp'), may hold values from 0.099609375 to 1.8984375
- w_query: bfloat16 [8192, 4096], P('seq', 'tp'), may hold values from -0.0625 to 0.0625
- w_kv: bfloat16 [8192, 2, 1024], P('seq', None, 'tp'), may hold values from -0.0625 to 0.0625
- b_query: float32 [4096], P('tp'), may hold values from -4 to 4
- b_kv: float32 [2, 1024], P(None, 'tp'), may hold values from -4 to 4
- kv_pool: bfloat16 [8192, 2, 8, 1024], P(('parts', 'seq'), None, None, 'tp'), parts along dimension 0, may hold values from -68 to 68
- prefix_pages: int32 [128, 32], P('parts'), parts along dimension 0, may hold values from 0 to 4095, as said below
- prefix_len: int32 [128], P('parts'), parts along dimension 0, may hold values from 0 to 256
- suffix_len: int32 [128], P('parts'), parts along dimension 0, may hold values from 1 to 128
- fresh_owner: int32 [2048, 1], P('parts'), parts along dimension 0, may hold values from 0 to 31; in each aligned block of 32 rows (0 to 31, 32 to 63, ...) at most 2 rows name the same one
Outputs:
- attn_out: bfloat16 [16384, 4096], P(('parts', 'seq'), 'tp'), parts along dimension 0
- fresh_pages: bfloat16 [4096, 2, 8, 1024], P(('parts', 'seq'), None, None, 'tp'), parts along dimension 0
There are 2 independent parts, one for each index of `parts`. A program takes and returns all parts, laid end to end along the dimension named above; an argument that names none is the same for every part. Nothing has to cross between parts.
Inputs may be any that keep to these rules, and one draw needn't show every extreme that they name: `prefix_pages`: page id q lies in the 128 pages of sequence group q // 128. Among the 64 entries of requests 2*g to 2*(g+1)-1, no group holds more than 3, and in every such block some group holds exactly 3. Entries past the matched prefix still name pages. `fresh_owner`: in the rows of one sequence group's requests (aligned blocks of 32 rows) no group is named more than 2 times; some blocks name one exactly 2 times.
All inputs are finite; a program needn't handle non-finite values.
Results may differ from a plain program's by a relative error of at most 0.005.
The roundings to bfloat16 on the way count: a program that leaves them out, or rounds other values in their place, can miss the bound.
Values may be sent and summed in bfloat16 or wider, within the bound.
No kernel may reach another device: no remote copies, remote signals or barrier semaphores. Data moves between devices by JAX's collectives and lax.ppermute only.
A program may use at most 64 MiB of HBM per device.

v0:
```python
import functools
import math

import jax
import jax.numpy as jnp
from jax import lax
from jax.experimental import pallas as pl
from jax.experimental.pallas import tpu as pltpu
from jax.sharding import PartitionSpec as P


HEAD_DIM = 128
BLOCK = 128
PAGE = 8
CORES = 2


def turn_tables(positions, width):
    half_dim = width // 2
    freq_index = jnp.arange(half_dim, dtype=jnp.float32)
    inverse = jnp.exp(freq_index * (-2.0 * math.log(1000000.0) / width))
    angles = positions.astype(jnp.float32)[:, None] * inverse
    cosine = jnp.cos(angles)
    sine = jnp.sin(angles)
    return cosine, sine


def attend(query, key_new, value_new, key_old, value_old, prefix_mine, suffix_mine):
    batch, block_len, heads_here, head_dim = query.shape
    kv_here = key_new.shape[2]
    group_size = heads_here // kv_here
    old_len = key_old.shape[1]
    grouped = query.reshape(batch, block_len, kv_here, group_size, head_dim)
    all_keys = jnp.concatenate([key_old, key_new], axis=1)
    all_values = jnp.concatenate([value_old, value_new], axis=1)
    scores = jnp.einsum(
        "btkgd,bskd->bkgts", grouped, all_keys, preferred_element_type=jnp.float32
    ) / math.sqrt(head_dim)
    key_pos = jnp.arange(old_len + block_len, dtype=jnp.int32)
    query_pos = jnp.arange(block_len, dtype=jnp.int32)
    in_prefix = key_pos[None, None, :] < prefix_mine[:, None, None]
    shifted = key_pos - old_len
    in_suffix = (shifted[None, None, :] <= query_pos[None, :, None]) & (
        shifted[None, None, :] < suffix_mine[:, None, None]
    )
    allowed = jnp.where(key_pos[None, None, :] < old_len, in_prefix, in_suffix)[:, None, None]
    masked = jnp.where(allowed, scores, -1e30)
    peak = jnp.max(masked, axis=-1, keepdims=True)
    weights = jnp.where(allowed, jnp.exp(masked - peak), 0.0)
    probs = (weights / jnp.sum(weights, axis=-1, keepdims=True)).astype(jnp.bfloat16)
    mixed = jnp.einsum("bkgts,bskd->btkgd", probs, all_values, preferred_element_type=jnp.float32)
    live = query_pos[None, :] < suffix_mine[:, None]
    mixed = jnp.where(live[:, :, None, None, None], mixed, 0.0)
    return mixed.reshape(batch * block_len, heads_here * head_dim).astype(jnp.bfloat16)


def swap_parts(value):
    count = lax.axis_size("parts")
    return lax.ppermute(value, "parts", [(i, i ^ 1) for i in range(count)])


def swap_cores(value):
    count = lax.axis_size("tp")
    return lax.ppermute(value, "tp", [(i, i ^ 1) for i in range(count)])


def shift_chips(value, by):
    count = lax.axis_size("tp")
    return lax.ppermute(value, "tp", [(i, (i + by * CORES) % count) for i in range(count)])


def gather_chips(own, cut):
    from_left = shift_chips(own, 1)
    from_right = shift_chips(own, -1)
    own_other = swap_cores(own)
    far_top = shift_chips(from_left[:cut], 1)
    far_low = shift_chips(from_right[cut:], -1)
    left_other = swap_cores(from_left)
    right_other = swap_cores(from_right)
    far = jnp.concatenate([far_top, far_low], axis=0)
    far_other = swap_cores(far)
    return (
        (own, own_other),
        (from_left, left_other),
        (from_right, right_other),
        (far, far_other),
    )


GAIN_ROWS = 16
STEPS = (0, -1, 1, 2)
STRIDE = 4


def shift_groups(value, by):
    count = lax.axis_size("seq")
    return lax.ppermute(value, "seq", [(i, (i + by) % count) for i in range(count)])


def gather_near(shard):
    count = lax.axis_size("seq")
    classes = [list(range(c, count, STRIDE)) for c in range(STRIDE)]
    return lax.all_gather(shard, "seq", axis=0, axis_index_groups=classes, tiled=True)


def trade_near(near):
    mid = near.shape[0] // 2
    return (
        near,
        shift_groups(near, -1),
        shift_groups(near, 1),
        shift_groups(near[:mid], 2),
        shift_groups(near[mid:], -2),
    )


CHUNK = 32


def pair_kernel(at_ref, *refs, count, shard):
    pieces = refs[:count]
    gains = refs[count : 2 * count]
    weights = refs[2 * count : 2 * count + 5]
    bias_ref, cos_ref, sin_ref, normed_ref, out_ref = refs[2 * count + 5 :]
    rows, feat = pieces[0].shape
    total = feat * len(pieces)

    def chunk(step, carry):
        row = pl.multiple_of(step * CHUNK, CHUNK)
        square = jnp.zeros((CHUNK, 1), jnp.float32)
        for piece in pieces:
            wide = piece[pl.ds(row, CHUNK), :].astype(jnp.float32)
            square = square + jnp.sum(wide * wide, axis=-1, keepdims=True)
        scale = lax.rsqrt(square / total + 1e-06)
        for k, piece in enumerate(pieces):
            wide = piece[pl.ds(row, CHUNK), :].astype(jnp.float32)
            gain = gains[k][:1, :].astype(jnp.float32)
            column = pl.multiple_of(at_ref[k] * feat, feat)
            normed_ref[pl.ds(row, CHUNK), pl.ds(column, feat)] = (wide * scale * gain).astype(
                jnp.bfloat16
            )
        return carry

    lax.fori_loop(0, rows // CHUNK, chunk, 0)
    half = weights[0].shape[0] // shard // 2
    acc = jnp.zeros(out_ref.shape, jnp.float32)
    for k, (weight, start) in enumerate(zip(weights, (0, 0, 0, 0, half))):
        for m in range(weight.shape[0] // shard):
            column = (at_ref[count + k] + STRIDE * (start + m)) * shard
            left = normed_ref[:, pl.ds(pl.multiple_of(column, shard), shard)]
            acc = acc + jnp.dot(
                left, weight[m * shard : (m + 1) * shard, :], preferred_element_type=jnp.float32
            )
    lin = acc + bias_ref[...]
    cosine = jnp.concatenate([cos_ref[...], cos_ref[...]], axis=1)
    sine = jnp.concatenate([-sin_ref[...], sin_ref[...]], axis=1)
    turned = lin * cosine + pltpu.roll(lin, lin.shape[1] // 2, 1) * sine
    out_ref[...] = turned.astype(jnp.bfloat16)


def project_pair(at, pieces, weights, shard, bias, cosine, sine):
    height, feat = pieces[0].shape
    tokens = height - GAIN_ROWS
    rows = tokens // 4
    width = weights[0].shape[1]
    whole = lambda a: pl.BlockSpec(a.shape, lambda i: (0, 0))
    by_rows = lambda w: pl.BlockSpec((rows, w), lambda i: (i, 0))
    gain_at = tokens // GAIN_ROWS
    return pl.pallas_call(
        functools.partial(pair_kernel, count=len(pieces), shard=shard),
        grid=(4,),
        in_specs=[pl.BlockSpec(memory_space=pltpu.SMEM)]
        + [by_rows(feat) for _ in pieces]
        + [pl.BlockSpec((GAIN_ROWS, feat), lambda i: (gain_at, 0)) for _ in pieces]
        + [whole(w) for w in weights]
        + [whole(bias), by_rows(width // 2), by_rows(width // 2)],
        out_specs=[by_rows(feat * len(pieces)), by_rows(width)],
        out_shape=[
            jax.ShapeDtypeStruct((tokens, feat * len(pieces)), jnp.bfloat16),
            jax.ShapeDtypeStruct((tokens, width), jnp.bfloat16),
        ],
    )(at, *pieces, *pieces, *weights, bias, cosine, sine)


def body(
    tokens,
    norm_gain,
    w_query,
    w_kv,
    b_query,
    b_kv,
    kv_pool,
    prefix_pages,
    prefix_len,
    suffix_len,
    fresh_owner,
):
    seq_count = lax.axis_size("seq")
    tp_count = lax.axis_size("tp")
    my_group = lax.axis_index("seq")
    my_tp = lax.axis_index("tp")
    parity = lax.axis_index("parts") % 2
    token_rows, feat = tokens.shape
    blocks_here = token_rows // BLOCK
    kv_width = w_kv.shape[2]
    kv_here = kv_width // HEAD_DIM
    query_width = w_query.shape[1]
    half_width = query_width // 2
    heads_here = query_width // HEAD_DIM
    half_heads = heads_here // 2
    pool_pages = kv_pool.shape[0]
    page_slots = prefix_pages.shape[1]
    prefix_entries = blocks_here * page_slots
    suffix_pages = BLOCK // PAGE
    fresh_entries = blocks_here * suffix_pages
    prefix_cap = max(3, prefix_entries // seq_count + 1)
    fresh_cap = max(2, (fresh_entries + seq_count - 1) // seq_count + 1)
    first_row = my_group * blocks_here
    prefix_mine = lax.dynamic_slice_in_dim(prefix_len, first_row, blocks_here)
    suffix_mine = lax.dynamic_slice_in_dim(suffix_len, first_row, blocks_here)
    w_query_half = lax.dynamic_slice_in_dim(w_query, parity * half_width, half_width, axis=1)
    w_query_half, w_kv = lax.optimization_barrier((w_query_half, w_kv))
    w_query_all = lax.all_gather(w_query_half, "seq", axis=0, tiled=True)
    w_pair_half = lax.dynamic_index_in_dim(w_kv, parity, 1, keepdims=False)
    w_pair_half, tokens, prefix_mine = lax.optimization_barrier((w_pair_half, tokens, prefix_mine))
    b_pair_half = lax.dynamic_index_in_dim(b_kv, parity, 0, keepdims=True)
    b_query_half = lax.dynamic_slice_in_dim(b_query, parity * half_width, half_width)[None]

    other_tokens = swap_parts(tokens)
    other_prefix = swap_parts(prefix_mine)
    w_pair_near = gather_near(w_pair_half)
    prefix_pages, fresh_owner, w_pair_near, other_tokens = lax.optimization_barrier(
        (prefix_pages, fresh_owner, w_pair_near, other_tokens)
    )
    owners_mine = lax.dynamic_slice_in_dim(
        fresh_owner[:, 0], first_row * suffix_pages, fresh_entries
    )
    w_pair_pieces = trade_near(w_pair_near)
    gain_rows = jnp.broadcast_to(norm_gain[None], (GAIN_ROWS, feat))
    both = jnp.concatenate([tokens, other_tokens, gain_rows], axis=0)
    pieces = gather_chips(both, token_rows)
    flat = [pair[core] for pair in pieces for core in range(CORES)]
    turns = jnp.array([step * CORES for step in STEPS for _ in range(CORES)], jnp.int32)
    cores = jnp.array([core for _ in STEPS for core in range(CORES)], jnp.int32)
    near_steps = jnp.array([0, 1, -1, 2, 2], jnp.int32)
    at = jnp.concatenate(
        [((my_tp + turns) % tp_count) ^ cores, (my_group + near_steps) % STRIDE]
    )

    all_ids = prefix_pages.reshape(seq_count, prefix_entries)
    all_owner = all_ids // pool_pages
    entry_ids = jnp.arange(prefix_entries, dtype=jnp.int32)
    before = (all_owner[:, :, None] == all_owner[:, None, :]) & (
        entry_ids[None, None, :] < entry_ids[None, :, None]
    )
    all_rank = jnp.sum(before.astype(jnp.int32), axis=-1)
    prefix_slots = jnp.arange(prefix_cap, dtype=jnp.int32)
    chosen = (all_owner[:, None, :] == my_group) & (
        all_rank[:, None, :] == prefix_slots[None, :, None]
    )
    picked = jnp.sum(jnp.where(chosen, entry_ids[None, None, :], 0), axis=-1)
    local_page = jnp.take_along_axis(all_ids, picked, axis=1) % pool_pages
    prefix_send = kv_pool[local_page]
    prefix_got = lax.all_to_all(prefix_send, "seq", split_axis=0, concat_axis=0, tiled=True)

    slot_ids = jnp.arange(BLOCK, dtype=jnp.int32)
    both_prefix = jnp.concatenate([prefix_mine, other_prefix])
    positions = (both_prefix[:, None] + slot_ids[None, :]).reshape(-1)
    live = (slot_ids[None, :] < suffix_mine[:, None])[:, :, None, None]
    cosine, sine = turn_tables(positions, HEAD_DIM)
    pair_cosine = jnp.where(parity == 0, cosine, 1.0)
    pair_sine = jnp.where(parity == 0, sine, 0.0)
    normed, pair_half = project_pair(
        at, flat, w_pair_pieces, w_kv.shape[0], b_pair_half.reshape(1, kv_width), pair_cosine, pair_sine
    )
    pair_half = pair_half.reshape(2 * blocks_here, BLOCK, kv_here, HEAD_DIM)
    pair_kept = pair_half[:blocks_here]
    pair_got = swap_parts(pair_half[blocks_here:])
    zero = jnp.zeros((), jnp.bfloat16)
    key_new = jnp.where(live, jnp.where(parity == 0, pair_kept, pair_got), zero)
    value_new = jnp.where(live, jnp.where(parity == 0, pair_got, pair_kept), zero)

    new_pages = jnp.stack(
        [
            key_new.reshape(fresh_entries, PAGE, kv_width),
            value_new.reshape(fresh_entries, PAGE, kv_width),
        ],
        axis=1,
    )
    fresh_ids = jnp.arange(fresh_entries, dtype=jnp.int32)
    fresh_before = (owners_mine[None, :] == owners_mine[:, None]) & (
        fresh_ids[None, :] < fresh_ids[:, None]
    )
    fresh_rank = jnp.sum(fresh_before.astype(jnp.int32), axis=1)
    group_ids = jnp.arange(seq_count, dtype=jnp.int32)
    fresh_slots = jnp.arange(fresh_cap, dtype=jnp.int32)
    placed = (owners_mine[None, None, :] == group_ids[:, None, None]) & (
        fresh_rank[None, None, :] == fresh_slots[None, :, None]
    )
    source = jnp.sum(jnp.where(placed, fresh_ids[None, None, :], 0), axis=-1)
    filled = jnp.any(placed, axis=-1)
    fresh_send = jnp.where(filled[:, :, None, None, None], new_pages[source], zero)
    fresh_got = lax.all_to_all(fresh_send, "seq", split_axis=0, concat_axis=0, tiled=True)

    query_lin = jnp.dot(normed, w_query_all, preferred_element_type=jnp.float32) + b_query_half
    query_lin = query_lin.reshape(2 * blocks_here * BLOCK, half_heads, HEAD_DIM)
    first, second = jnp.split(query_lin, 2, axis=-1)
    query_half = jnp.concatenate(
        [
            first * cosine[:, None, :] - second * sine[:, None, :],
            second * cosine[:, None, :] + first * sine[:, None, :],
        ],
        axis=-1,
    )
    query_half = query_half.astype(jnp.bfloat16)
    query_half = query_half.reshape(2 * blocks_here, BLOCK, half_heads, HEAD_DIM)
    query_kept = query_half[:blocks_here]
    query_got = swap_parts(query_half[blocks_here:])
    query = jnp.concatenate(
        [
            jnp.where(parity == 0, query_kept, query_got),
            jnp.where(parity == 0, query_got, query_kept),
        ],
        axis=2,
    )

    my_rank = lax.dynamic_index_in_dim(all_rank, my_group, 0, keepdims=False)
    my_ids = lax.dynamic_index_in_dim(all_ids, my_group, 0, keepdims=False)
    arrived_at = my_ids // pool_pages * prefix_cap + my_rank
    fetched = prefix_got.reshape(seq_count * prefix_cap, 2, PAGE, kv_width)[arrived_at]
    fetched = fetched.reshape(blocks_here, page_slots, 2, PAGE, kv_here, HEAD_DIM)
    key_old = fetched[:, :, 0].reshape(blocks_here, page_slots * PAGE, kv_here, HEAD_DIM)
    value_old = fetched[:, :, 1].reshape(blocks_here, page_slots * PAGE, kv_here, HEAD_DIM)
    attn_out = attend(query, key_new, value_new, key_old, value_old, prefix_mine, suffix_mine)
    fresh_out = fresh_got.reshape(seq_count * fresh_cap, 2, PAGE, kv_width)
    return (attn_out, fresh_out)


def solution(mesh):
    placed = (
        P(("parts", "seq"), "tp"),
        P("tp"),
        P("seq", "tp"),
        P("seq", None, "tp"),
        P("tp"),
        P(None, "tp"),
        P(("parts", "seq"), None, None, "tp"),
        P("parts", None),
        P("parts"),
        P("parts"),
        P("parts", None),
    )

    return jax.shard_map(
        body,
        mesh=mesh,
        in_specs=placed,
        out_specs=(P(("parts", "seq"), "tp"), P(("parts", "seq"), None, None, "tp")),
        check_vma=False,
    )
```

profile of v0, /device:TPU:40, one launch (start us, length us, event | category | flops | bytes accessed | tf_op | source)
XLA Modules:
  0.0 302.4 jit_solution(417687119907988468)
XLA Ops:
  7.3 1.7 constant_dynamic-slice_fusion.4
  9.0 0.9 copy.42
  10.0 0.7 dynamic_slice.33
  10.7 41.8 %collective-permute-start = (bf16[256,1024]{1,0:T(8,128)(2,1)}, bf16[256,1024]{1,0:T(8,128)(2,1)S(1)}, u32[]{:S(2)}, u32[]{:S(2)}) collective-permute-start(bf16[256,1024]{1,0:T(8,128)(2,1)} %param.14), channel_id=1, source_target_pairs={{0,256},{256,0},{1,257},{257,1},{2,258},{258,2},{3,259},{259,3},{4... | collective-permute-start | bytes 1572872 | tf_op jit(solution)/shard_map/ppermute | solution.py:59
  52.6 2.0 collective-permute-start.13
  54.5 0.7 dynamic_slice.30
  55.3 0.7 fusion.21
  56.1 0.1 iota_compare_fusion
  56.2 41.5 %all_gather.6.refs_16_ = bf16[2048,128]{1,0:T(8,128)(2,1)S(1)} all-gather(bf16[256,128]{1,0:T(8,128)(2,1)S(1)} %dynamic-slice_bitcast_fusion), channel_id=1, replica_groups={{0,32,64,96,128,160,192,224},{8,40,72,104,136,168,200,232},{16,48,80,11..., dimensions={0}, use_global_device_ids=true | all-gather | bytes 589824 | tf_op jit(solution)/shard_map/all_gather | solution.py:103
  97.7 0.7 broadcast_in_dim.166
  98.5 4.9 %collective-permute-start.2 = (bf16[528,1024]{1,0:T(8,128)(2,1)S(1)}, bf16[528,1024]{1,0:T(8,128)(2,1)}, u32[]{:S(2)}, u32[]{:S(2)}) collective-permute-start(bf16[528,1024]{1,0:T(8,128)(2,1)S(1)} %pad_maximum_fusion.refs_0_.refs_8_), channel_id=1, source_target_pairs={{0,2},{1,3},{2,4},{3,5},{4,6},{5,7},{6,0},{7,1},{8,10},{9,11},{10,... | collective-permute-start | bytes 3244040 | tf_op jit(solution)/shard_map/ppermute | solution.py:69
  103.4 2.3 collective-permute-start.4
  105.9 0.9 convert_reduce_fusion
  106.8 0.1 select_reduce_fusion
  107.2 1.3 gather_fusion.3
  108.9 0.7 fusion.26
  109.6 0.2 convert_reduce_fusion.1
  110.2 1.4 gather_fusion
  111.6 17.1 %all-to-all-start = ((bf16[32,3,2,8,128]{4,3,2,1,0:T(8,128)(2,1)}), bf16[32,3,2,8,128]{4,3,2,1,0:T(8,128)(2,1)}, u32[]{:S(2)}, u32[]{:S(2)}) async-start(bf16[32,3,2,8,128]{4,3,2,1,0:T(8,128)(2,1)} %bitcast.95), calls=%async_computation | async-start | bytes 786432 | tf_op jit(solution)/shard_map/all_to_all | solution.py:264
  128.8 1.1 slice.65
  129.9 2.0 collective-permute-start.6
  132.0 5.1 %collective-permute-start.7 = (bf16[272,1024]{1,0:T(8,128)(2,1)S(1)}, bf16[272,1024]{1,0:T(8,128)(2,1)S(1)}, u32[]{:S(2)}, u32[]{:S(2)}) collective-permute-start(bf16[272,1024]{1,0:T(8,128)(2,1)S(1)} %slice.66), channel_id=1, source_target_pairs={{0,6},{1,7},{2,0},{3,1},{4,2},{5,3},{6,4},{7,5},{8,14},{9,15},{10,... | collective-permute-start | bytes 1671176 | tf_op jit(solution)/shard_map/ppermute | solution.py:69
  137.2 4.2 %collective-permute-start.11 = (bf16[1024,128]{1,0:T(8,128)(2,1)S(1)}, bf16[1024,128]{1,0:T(8,128)(2,1)S(1)}, u32[]{:S(2)}, u32[]{:S(2)}) collective-permute-start(bf16[1024,128]{1,0:T(8,128)(2,1)S(1)} %get-tuple-element.33), channel_id=1, source_target_pairs={{0,16},{8,24},{16,32},{24,40},{32,48},{40,56},{48,64},{56,72},{64,... | collective-permute-start | bytes 786440 | tf_op jit(solution)/shard_map/ppermute | solution.py:97
  141.4 3.9 %collective-permute-start.12 = (bf16[1024,128]{1,0:T(8,128)(2,1)S(1)}, bf16[1024,128]{1,0:T(8,128)(2,1)S(1)}, u32[]{:S(2)}, u32[]{:S(2)}) collective-permute-start(bf16[1024,128]{1,0:T(8,128)(2,1)S(1)} %get-tuple-element.32), channel_id=1, source_target_pairs={{0,240},{8,248},{16,0},{24,8},{32,16},{40,24},{48,32},{56,40},{64,... | collective-permute-start | bytes 786440 | tf_op jit(solution)/shard_map/ppermute | solution.py:97
  145.3 2.0 collective-permute-start.1
  147.2 0.8 constant_dynamic-update-slice_fusion.1
  148.1 3.2 %collective-permute-start.10 = (bf16[2048,128]{1,0:T(8,128)(2,1)S(1)}, bf16[2048,128]{1,0:T(8,128)(2,1)}, u32[]{:S(2)}, u32[]{:S(2)}) collective-permute-start(bf16[2048,128]{1,0:T(8,128)(2,1)S(1)} %all_gather.6.refs_16_), channel_id=1, source_target_pairs={{0,8},{8,16},{16,24},{24,32},{32,40},{40,48},{48,56},{56,64},{64,7... | collective-permute-start | bytes 1572872 | tf_op jit(solution)/shard_map/ppermute | solution.py:97
  151.3 0.8 constant_dynamic-update-slice_fusion.refs_6_.refs_14_
  152.2 2.1 collective-permute-start.3
  154.3 28.4 %collective-permute-done.11.refs_19_ = bf16[1024,128]{1,0:T(8,128)(2,1)S(1)} collective-permute-done((bf16[1024,128]{1,0:T(8,128)(2,1)S(1)}, bf16[1024,128]{1,0:T(8,128)(2,1)S(1)}, u32[]{:S(2)}, u32[]{:S(2)}) %collective-permute-start.11) | collective-permute-done | bytes 262176 | tf_op jit(solution)/shard_map/ppermute | solution.py:97
  182.8 1.9 collective-permute-start.5
  184.7 0.7 copy-done.8
  185.4 2.4 collective-permute-start.8
  187.9 0.6 constant_dynamic-slice_fusion.1.refs_21_
  188.5 0.6 dynamic_slice.37
  189.1 0.6 pad_add_fusion.at_ref
  189.7 1.0 and_select_fusion
  190.8 8.2 %collective-permute-done.10.refs_18_ = bf16[2048,128]{1,0:T(8,128)(2,1)} collective-permute-done((bf16[2048,128]{1,0:T(8,128)(2,1)S(1)}, bf16[2048,128]{1,0:T(8,128)(2,1)}, u32[]{:S(2)}, u32[]{:S(2)}) %collective-permute-start.10) | collective-permute-done | bytes 524320 | tf_op jit(solution)/shard_map/ppermute | solution.py:97
  198.9 3.2 %collective-permute-start.9 = (bf16[2048,128]{1,0:T(8,128)(2,1)S(1)}, bf16[2048,128]{1,0:T(8,128)(2,1)}, u32[]{:S(2)}, u32[]{:S(2)}) collective-permute-start(bf16[2048,128]{1,0:T(8,128)(2,1)S(1)} %all_gather.6.refs_16_), channel_id=1, source_target_pairs={{0,248},{8,0},{16,8},{24,16},{32,24},{40,32},{48,40},{56,48},{64,5... | collective-permute-start | bytes 1572872 | tf_op jit(solution)/shard_map/ppermute | solution.py:97
  202.2 1.9 multiply_cosine_fusion
  204.3 10.5 %collective-permute-done.9.refs_17_ = bf16[2048,128]{1,0:T(8,128)(2,1)} collective-permute-done((bf16[2048,128]{1,0:T(8,128)(2,1)S(1)}, bf16[2048,128]{1,0:T(8,128)(2,1)}, u32[]{:S(2)}, u32[]{:S(2)}) %collective-permute-start.9) | collective-permute-done | bytes 524320 | tf_op jit(solution)/shard_map/ppermute | solution.py:97
  214.9 12.1 %shard_map.149 = (bf16[512,8192]{1,0:T(8,128)(2,1)}, bf16[512,128]{1,0:T(8,128)(2,1)}) custom-call(s32[13]{0:T(128)} %pad_add_fusion.at_ref, bf16[528,1024]{1,0:T(8,128)(2,1)} %copy-done.1, bf16[528,1024]{1,0:T(8,128)(2,1)} %collective-permute-done.1.refs_1_.refs_9_, bf16[528,1024]{1,0:T(8,128)(2,1)} %collective-permute-done.2.refs_2_.refs_10_, ...), custom_call_target="tpu_custom_call" | custom-call | tf_op jit(solution)/shard_map/pallas_call | solution.py:169
  227.0 0.9 fusion.33
  227.9 2.0 collective-permute-start.14
  229.9 4.2 %collective-permute-done.14 = bf16[2,128,1,128]{3,1,0,2:T(8,128)(2,1)S(1)} collective-permute-done((bf16[2,128,1,128]{3,1,0,2:T(8,128)(2,1)S(1)}, bf16[2,128,1,128]{3,1,0,2:T(8,128)(2,1)S(1)}, u32[]{:S(2)}, u32[]{:S(2)}) %collective-permute-start.14) | collective-permute-done | bytes 65568 | tf_op jit(solution)/shard_map/ppermute | solution.py:59
  234.2 0.7 gather_fusion.2
  234.9 0.8 broadcast_select_fusion
  235.7 17.9 %all-to-all-start.1 = ((bf16[32,2,2,8,128]{4,3,2,1,0:T(8,128)(2,1)}), bf16[32,2,2,8,128]{4,3,2,1,0:T(8,128)(2,1)S(1)}, u32[]{:S(2)}, u32[]{:S(2)}) async-start(bf16[32,2,2,8,128]{4,3,2,1,0:T(8,128)(2,1)} %broadcast_select_fusion), calls=%async_computation.1 | async-start | bytes 524288 | tf_op jit(solution)/shard_map/all_to_all | solution.py:303
  253.6 0.1 copy.49
  253.7 1.6 gather_fusion.1
  255.4 6.9 %convolution_add_fusion = f32[512,256]{0,1:T(8,128)S(1)} fusion(bf16[512,8192]{1,0:T(8,128)(2,1)} %get-tuple-element.21, bf16[8192,256]{1,0:T(8,128)(2,1)} %all-gather.2.cloned.1.call-done, f32[256]{0:T(256)S(1)} %copy-done.10), kind=kOutput, calls=%fused_computation.9 | convolution fusion | flops 2147614720 | bytes 13108224 | tf_op jit(solution)/shard_map/dot_general | solution.py:305
  262.4 0.2 copy.65
  262.6 0.2 copy.66
  262.8 0.5 copy-done.4
  263.3 0.1 subtract_convert_fusion
  263.5 0.1 fusion.13
  263.6 2.0 collective-permute-start.15
  265.8 26.8 %all-to-all-done.1 = bf16[32,2,2,8,128]{4,3,2,1,0:T(8,128)(2,1)S(1)} async-done(((bf16[32,2,2,8,128]{4,3,2,1,0:T(8,128)(2,1)}), bf16[32,2,2,8,128]{4,3,2,1,0:T(8,128)(2,1)S(1)}, u32[]{:S(2)}, u32[]{:S(2)}) %all-to-all-start.1) | async-done | bytes 262176 | tf_op jit(solution)/shard_map/all_to_all | solution.py:303
  292.7 0.4 fusion.34
  293.1 0.3 fusion
  293.4 0.5 fusion.3
  293.9 0.2 copy.57
  294.1 0.7 copy.71
  294.9 0.7 copy.74
  (89 shorter events, 2.5 us)
Async XLA Ops:
  7.2 103.0 %copy-start = (bf16[128,2,8,128]{3,2,1,0:T(8,128)(2,1)S(1)}, bf16[128,2,8,128]{3,2,1,0:T(8,128)(2,1)}, u32[]{:S(2)}) copy-start(bf16[128,2,8,128]{3,2,1,0:T(8,128)(2,1)} %param.20) | copy-start | bytes 1572868
  7.2 91.2 %copy-start.5 = (bf16[256,1024]{1,0:T(8,128)(2,1)S(1)}, bf16[256,1024]{1,0:T(8,128)(2,1)}, u32[]{:S(2)}) copy-start(bf16[256,1024]{1,0:T(8,128)(2,1)} %param.14) | copy-start | bytes 1572868
  7.2 248.2 %all-gather.2.cloned.1.call-start = ((), (), s32[]{:S(2)}) async-start(), calls=%async_computation.2 | async-start | bytes 4325376 | tf_op jit(solution)/shard_map/all_gather | solution.py:223
  10.0 95.7 %copy-start.9 = (s32[64,32]{0,1:T(8,128)S(1)}, s32[64,32]{0,1:T(8,128)}, u32[]{:S(2)}) copy-start(s32[64,32]{0,1:T(8,128)} %param.21) | copy-start | bytes 24580
  10.7 87.0 %collective-permute-start = (bf16[256,1024]{1,0:T(8,128)(2,1)}, bf16[256,1024]{1,0:T(8,128)(2,1)S(1)}, u32[]{:S(2)}, u32[]{:S(2)}) collective-permute-start(bf16[256,1024]{1,0:T(8,128)(2,1)} %param.14), channel_id=1, source_target_pairs={{0,256},{256,0},{1,257},{257,1},{2,258},{258,2},{3,259},{259,3},{4... | collective-permute-start | bytes 1572872 | tf_op jit(solution)/shard_map/ppermute | solution.py:59
  52.6 99.6 %collective-permute-start.13 = (s32[2]{0:T(128)S(1)}, s32[2]{0:T(128)S(1)}, u32[]{:S(2)}, u32[]{:S(2)}) collective-permute-start(s32[2]{0:T(128)S(1)} %dynamic_slice.33), channel_id=1, source_target_pairs={{0,256},{256,0},{1,257},{257,1},{2,258},{258,2},{3,259},{259,3},{4... | collective-permute-start | bytes 32 | tf_op jit(solution)/shard_map/ppermute | solution.py:59
  97.7 101.2 %copy-start.3 = (bf16[2048,128]{1,0:T(8,128)(2,1)}, bf16[2048,128]{1,0:T(8,128)(2,1)S(1)}, u32[]{:S(2)}) copy-start(bf16[2048,128]{1,0:T(8,128)(2,1)S(1)} %all_gather.6.refs_16_) | copy-start | bytes 1572868
  98.5 46.7 %copy-start.1 = (bf16[528,1024]{1,0:T(8,128)(2,1)}, bf16[528,1024]{1,0:T(8,128)(2,1)S(1)}, u32[]{:S(2)}) copy-start(bf16[528,1024]{1,0:T(8,128)(2,1)S(1)} %pad_maximum_fusion.refs_0_.refs_8_) | copy-start | bytes 3244036
  98.5 30.3 %collective-permute-start.2 = (bf16[528,1024]{1,0:T(8,128)(2,1)S(1)}, bf16[528,1024]{1,0:T(8,128)(2,1)}, u32[]{:S(2)}, u32[]{:S(2)}) collective-permute-start(bf16[528,1024]{1,0:T(8,128)(2,1)S(1)} %pad_maximum_fusion.refs_0_.refs_8_), channel_id=1, source_target_pairs={{0,2},{1,3},{2,4},{3,5},{4,6},{5,7},{6,0},{7,1},{8,10},{9,11},{10,... | collective-permute-start | bytes 3244040 | tf_op jit(solution)/shard_map/ppermute | solution.py:69
  103.4 28.5 %collective-permute-start.4 = (bf16[528,1024]{1,0:T(8,128)(2,1)S(1)}, bf16[528,1024]{1,0:T(8,128)(2,1)S(1)}, u32[]{:S(2)}, u32[]{:S(2)}) collective-permute-start(bf16[528,1024]{1,0:T(8,128)(2,1)S(1)} %pad_maximum_fusion.refs_0_.refs_8_), channel_id=1, source_target_pairs={{0,6},{1,7},{2,0},{3,1},{4,2},{5,3},{6,4},{7,5},{8,14},{9,15},{10,... | collective-permute-start | bytes 3244040 | tf_op jit(solution)/shard_map/ppermute | solution.py:69
  108.5 23.4 %copy-start.15 = (s32[5]{0:T(128)S(1)}, s32[5]{0:T(128)}, u32[]{:S(2)}) copy-start(s32[5]{0:T(128)} %constant.168.clone) | copy-start | bytes 64
  111.6 124.1 %all-to-all-start = ((bf16[32,3,2,8,128]{4,3,2,1,0:T(8,128)(2,1)}), bf16[32,3,2,8,128]{4,3,2,1,0:T(8,128)(2,1)}, u32[]{:S(2)}, u32[]{:S(2)}) async-start(bf16[32,3,2,8,128]{4,3,2,1,0:T(8,128)(2,1)} %bitcast.95), calls=%async_computation | async-start | bytes 786432 | tf_op jit(solution)/shard_map/all_to_all | solution.py:264
  128.8 105.2 %copy-start.11 = (pred[2,128]{1,0:T(4,128)(4,1)}, pred[2,128]{1,0:T(4,128)(4,1)S(1)}, u32[]{:S(2)}) copy-start(pred[2,128]{1,0:T(4,128)(4,1)S(1)} %iota_compare_fusion.8) | copy-start | bytes 772
  129.9 15.3 %collective-permute-start.6 = (bf16[256,1024]{1,0:T(8,128)(2,1)S(1)}, bf16[256,1024]{1,0:T(8,128)(2,1)S(1)}, u32[]{:S(2)}, u32[]{:S(2)}) collective-permute-start(bf16[256,1024]{1,0:T(8,128)(2,1)S(1)} %slice.65), channel_id=1, source_target_pairs={{0,2},{1,3},{2,4},{3,5},{4,6},{5,7},{6,0},{7,1},{8,10},{9,11},{10,... | collective-permute-start | bytes 1572872 | tf_op jit(solution)/shard_map/ppermute | solution.py:69
  131.9 50.8 %copy-start.2 = (bf16[528,1024]{1,0:T(8,128)(2,1)}, bf16[528,1024]{1,0:T(8,128)(2,1)S(1)}, u32[]{:S(2)}) copy-start(bf16[528,1024]{1,0:T(8,128)(2,1)S(1)} %collective-permute-done.4.refs_4_.refs_12_) | copy-start | bytes 3244036
  132.0 16.1 %collective-permute-start.7 = (bf16[272,1024]{1,0:T(8,128)(2,1)S(1)}, bf16[272,1024]{1,0:T(8,128)(2,1)S(1)}, u32[]{:S(2)}, u32[]{:S(2)}) collective-permute-start(bf16[272,1024]{1,0:T(8,128)(2,1)S(1)} %slice.66), channel_id=1, source_target_pairs={{0,6},{1,7},{2,0},{3,1},{4,2},{5,3},{6,4},{7,5},{8,14},{9,15},{10,... | collective-permute-start | bytes 1671176 | tf_op jit(solution)/shard_map/ppermute | solution.py:69
  137.1 50.7 %copy-start.14 = (f32[2,128]{1,0:T(2,128)S(1)}, f32[2,128]{1,0:T(2,128)}, u32[]{:S(2)}) copy-start(f32[2,128]{1,0:T(2,128)} %param.19) | copy-start | bytes 3076
  137.1 51.3 %copy-start.13 = (f32[512]{0:T(512)S(1)}, f32[512]{0:T(512)}, u32[]{:S(2)}) copy-start(f32[512]{0:T(512)} %param.18) | copy-start | bytes 6148
  137.2 45.5 %collective-permute-start.11 = (bf16[1024,128]{1,0:T(8,128)(2,1)S(1)}, bf16[1024,128]{1,0:T(8,128)(2,1)S(1)}, u32[]{:S(2)}, u32[]{:S(2)}) collective-permute-start(bf16[1024,128]{1,0:T(8,128)(2,1)S(1)} %get-tuple-element.33), channel_id=1, source_target_pairs={{0,16},{8,24},{16,32},{24,40},{32,48},{40,56},{48,64},{56,72},{64,... | collective-permute-start | bytes 786440 | tf_op jit(solution)/shard_map/ppermute | solution.py:97
  141.4 43.3 %collective-permute-start.12 = (bf16[1024,128]{1,0:T(8,128)(2,1)S(1)}, bf16[1024,128]{1,0:T(8,128)(2,1)S(1)}, u32[]{:S(2)}, u32[]{:S(2)}) collective-permute-start(bf16[1024,128]{1,0:T(8,128)(2,1)S(1)} %get-tuple-element.32), channel_id=1, source_target_pairs={{0,240},{8,248},{16,0},{24,8},{32,16},{40,24},{48,32},{56,40},{64,... | collective-permute-start | bytes 786440 | tf_op jit(solution)/shard_map/ppermute | solution.py:97
  145.3 69.6 %collective-permute-start.1 = (bf16[528,1024]{1,0:T(8,128)(2,1)S(1)}, bf16[528,1024]{1,0:T(8,128)(2,1)}, u32[]{:S(2)}, u32[]{:S(2)}) collective-permute-start(bf16[528,1024]{1,0:T(8,128)(2,1)S(1)} %pad_maximum_fusion.refs_0_.refs_8_), channel_id=1, source_target_pairs={{0,1},{1,0},{2,3},{3,2},{4,5},{5,4},{6,7},{7,6},{8,9},{9,8},{10,11... | collective-permute-start | bytes 3244040 | tf_op jit(solution)/shard_map/ppermute | solution.py:64
  148.1 50.9 %collective-permute-start.10 = (bf16[2048,128]{1,0:T(8,128)(2,1)S(1)}, bf16[2048,128]{1,0:T(8,128)(2,1)}, u32[]{:S(2)}, u32[]{:S(2)}) collective-permute-start(bf16[2048,128]{1,0:T(8,128)(2,1)S(1)} %all_gather.6.refs_16_), channel_id=1, source_target_pairs={{0,8},{8,16},{16,24},{24,32},{32,40},{40,48},{48,56},{56,64},{64,7... | collective-permute-start | bytes 1572872 | tf_op jit(solution)/shard_map/ppermute | solution.py:97
  152.2 62.7 %collective-permute-start.3 = (bf16[528,1024]{1,0:T(8,128)(2,1)}, bf16[528,1024]{1,0:T(8,128)(2,1)}, u32[]{:S(2)}, u32[]{:S(2)}) collective-permute-start(bf16[528,1024]{1,0:T(8,128)(2,1)} %collective-permute-done.2.refs_2_.refs_10_), channel_id=1, source_target_pairs={{0,1},{1,0},{2,3},{3,2},{4,5},{5,4},{6,7},{7,6},{8,9},{9,8},{10,11... | collective-permute-start | bytes 3244040 | tf_op jit(solution)/shard_map/ppermute | solution.py:64
  182.8 2.0 copy-start.7
  182.8 32.1 %collective-permute-start.5 = (bf16[528,1024]{1,0:T(8,128)(2,1)S(1)}, bf16[528,1024]{1,0:T(8,128)(2,1)}, u32[]{:S(2)}, u32[]{:S(2)}) collective-permute-start(bf16[528,1024]{1,0:T(8,128)(2,1)S(1)} %collective-permute-done.4.refs_4_.refs_12_), channel_id=1, source_target_pairs={{0,1},{1,0},{2,3},{3,2},{4,5},{5,4},{6,7},{7,6},{8,9},{9,8},{10,11... | collective-permute-start | bytes 3244040 | tf_op jit(solution)/shard_map/ppermute | solution.py:64
  184.7 0.7 copy-start.8
  185.4 29.4 %collective-permute-start.8 = (bf16[528,1024]{1,0:T(8,128)(2,1)}, bf16[528,1024]{1,0:T(8,128)(2,1)}, u32[]{:S(2)}, u32[]{:S(2)}) collective-permute-start(bf16[528,1024]{1,0:T(8,128)(2,1)} %constant_dynamic-update-slice_fusion.refs_6_.refs_14_), channel_id=1, source_target_pairs={{0,1},{1,0},{2,3},{3,2},{4,5},{5,4},{6,7},{7,6},{8,9},{9,8},{10,11... | collective-permute-start | bytes 3244040 | tf_op jit(solution)/shard_map/ppermute | solution.py:64
  198.9 15.9 %collective-permute-start.9 = (bf16[2048,128]{1,0:T(8,128)(2,1)S(1)}, bf16[2048,128]{1,0:T(8,128)(2,1)}, u32[]{:S(2)}, u32[]{:S(2)}) collective-permute-start(bf16[2048,128]{1,0:T(8,128)(2,1)S(1)} %all_gather.6.refs_16_), channel_id=1, source_target_pairs={{0,248},{8,0},{16,8},{24,16},{32,24},{40,32},{48,40},{56,48},{64,5... | collective-permute-start | bytes 1572872 | tf_op jit(solution)/shard_map/ppermute | solution.py:97
  227.0 28.4 %copy-start.10 = (f32[256]{0:T(256)S(1)}, f32[256]{0:T(256)}, u32[]{:S(2)}) copy-start(f32[256]{0:T(256)} %dynamic_slice.37) | copy-start | bytes 3076
  227.9 6.2 %collective-permute-start.14 = (bf16[2,128,1,128]{3,1,0,2:T(8,128)(2,1)S(1)}, bf16[2,128,1,128]{3,1,0,2:T(8,128)(2,1)S(1)}, u32[]{:S(2)}, u32[]{:S(2)}) collective-permute-start(bf16[2,128,1,128]{3,1,0,2:T(8,128)(2,1)S(1)} %bitcast.107), channel_id=1, source_target_pairs={{0,256},{256,0},{1,257},{257,1},{2,258},{258,2},{3,259},{259,3},{4... | collective-permute-start | bytes 196616 | tf_op jit(solution)/shard_map/ppermute | solution.py:59
  235.7 56.9 %all-to-all-start.1 = ((bf16[32,2,2,8,128]{4,3,2,1,0:T(8,128)(2,1)}), bf16[32,2,2,8,128]{4,3,2,1,0:T(8,128)(2,1)S(1)}, u32[]{:S(2)}, u32[]{:S(2)}) async-start(bf16[32,2,2,8,128]{4,3,2,1,0:T(8,128)(2,1)} %broadcast_select_fusion), calls=%async_computation.1 | async-start | bytes 524288 | tf_op jit(solution)/shard_map/all_to_all | solution.py:303
  262.4 1.0 copy-start.4
  263.4 29.2 %copy-start.6 = (pred[2,128,384]{1,2,0:T(8,128)(4,1)S(1)}, pred[2,128,384]{1,2,0:T(8,128)(4,1)}, u32[]{:S(2)}) copy-start(pred[2,128,384]{1,2,0:T(8,128)(4,1)} %and_select_fusion) | copy-start | bytes 294916
  263.6 29.0 %collective-permute-start.15 = (bf16[2,128,2,128]{3,1,2,0:T(8,128)(2,1)S(1)}, bf16[2,128,2,128]{3,1,2,0:T(8,128)(2,1)S(1)}, u32[]{:S(2)}, u32[]{:S(2)}) collective-permute-start(bf16[2,128,2,128]{3,1,2,0:T(8,128)(2,1)S(1)} %copy.53), channel_id=1, source_target_pairs={{0,256},{256,0},{1,257},{257,1},{2,258},{258,2},{3,259},{259,3},{4... | collective-permute-start | bytes 393224 | tf_op jit(solution)/shard_map/ppermute | solution.py:59
  292.7 0.7 copy-start.12
Sparse Core Ops, SparseCore 0:
  10.1 203.5 all-gather.1
where the time goes:
time: 303 us; the launch traced here: 302 us
  starting transfers between devices  120 us (40%)
  waiting for transfers between devices  78.2 us (26%)
  blocking collectives  41.5 us (14%)
  local copies, waits for them, and re-layouts  20 us (7%)
  between operations  14.7 us (5%)
  Pallas kernels  12.1 us (4%)
  other arithmetic  7.94 us (3%)
  matrix products  7.86 us (3%)
    ppermute x4, starting transfers between devices, swap_parts(): return lax.ppermute(value, 'parts', [(i, i ^ 1) for i in range(count)])  47.8 us
    ppermute x4, waiting for transfers between devices, shift_groups(): lax.ppermute(value, 'seq', [(i, (i + by) % count) for i in range(count)])  47.1 us
    all_gather x1, blocking collectives, gather_near(): lax.all_gather(shard, 'seq', axis=0, axis_index_groups=classes, tiled=True)  41.5 us
    all_to_all x1, waiting for transfers between devices, body(): lax.all_to_all(fresh_send, 'seq', split_axis=0, concat_axis=0, tiled=True)  26.8 us
    all_to_all x1, starting transfers between devices, body(): lax.all_to_all(fresh_send, 'seq', split_axis=0, concat_axis=0, tiled=True)  17.9 us
    all_to_all x1, starting transfers between devices, body(): lax.all_to_all(prefix_send, 'seq', split_axis=0, concat_axis=0, tiled=True)  17.1 us
    ppermute x4, starting transfers between devices, shift_groups(): lax.ppermute(value, 'seq', [(i, (i + by) % count) for i in range(count)])  14.4 us
    ppermute x4, starting transfers between devices, shift_chips(): lax.ppermute(value, 'tp', [(i, (i + by * CORES) % count) for i in range(c...  14.3 us
  transfers between devices with their start and end apart: 19, of which 5 were waited for; matrix products, arithmetic and copies ran while one was open for 10% of the time, Pallas kernels for 4%

commit v1 on v0

--- a/solution.py
+++ b/solution.py
@@ -229,11 +229,8 @@
     other_tokens = swap_parts(tokens)
     other_prefix = swap_parts(prefix_mine)
     w_pair_near = gather_near(w_pair_half)
-    prefix_pages, fresh_owner, w_pair_near, other_tokens = lax.optimization_barrier(
-        (prefix_pages, fresh_owner, w_pair_near, other_tokens)
-    )
-    owners_mine = lax.dynamic_slice_in_dim(
-        fresh_owner[:, 0], first_row * suffix_pages, fresh_entries
+    prefix_pages, w_pair_near, other_tokens = lax.optimization_barrier(
+        (prefix_pages, w_pair_near, other_tokens)
     )
     w_pair_pieces = trade_near(w_pair_near)
     gain_rows = jnp.broadcast_to(norm_gain[None], (GAIN_ROWS, feat))
@@ -261,6 +258,10 @@
     picked = jnp.sum(jnp.where(chosen, entry_ids[None, None, :], 0), axis=-1)
     local_page = jnp.take_along_axis(all_ids, picked, axis=1) % pool_pages
     prefix_send = kv_pool[local_page]
+    fresh_owner, prefix_send = lax.optimization_barrier((fresh_owner, prefix_send))
+    owners_mine = lax.dynamic_slice_in_dim(
+        fresh_owner[:, 0], first_row * suffix_pages, fresh_entries
+    )
     prefix_got = lax.all_to_all(prefix_send, "seq", split_axis=0, concat_axis=0, tiled=True)
 
     slot_ids = jnp.arange(BLOCK, dtype=jnp.int32)

time: 303 us -> 307 us (1.013)
  the two profiles are of different devices: /device:TPU:40 before, /device:TPU:34 now
where the time goes in v1:
time: 307 us; the launch traced here: 306 us
  starting transfers between devices  85 us (28%)
  blocking collectives  80 us (26%)
  waiting for transfers between devices  77.5 us (25%)
  local copies, waits for them, and re-layouts  20 us (7%)
  between operations  14.7 us (5%)
  Pallas kernels  12.1 us (4%)
  other arithmetic  8.59 us (3%)
  matrix products  7.86 us (3%)
    all_gather x1, blocking collectives, gather_near(): lax.all_gather(shard, 'seq', axis=0, axis_index_groups=classes, tiled=True)  80 us
    ppermute x4, waiting for transfers between devices, shift_groups(): lax.ppermute(value, 'seq', [(i, (i + by) % count) for i in range(count)])  49.6 us
    all_to_all x1, waiting for transfers between devices, body(): lax.all_to_all(fresh_send, 'seq', split_axis=0, concat_axis=0, tiled=True)  25.6 us
    all_to_all x1, starting transfers between devices, body(): lax.all_to_all(fresh_send, 'seq', split_axis=0, concat_axis=0, tiled=True)  18.5 us
    all_to_all x1, starting transfers between devices, body(): lax.all_to_all(prefix_send, 'seq', split_axis=0, concat_axis=0, tiled=True)  17.5 us
    ppermute x4, starting transfers between devices, shift_groups(): lax.ppermute(value, 'seq', [(i, (i + by) % count) for i in range(count)])  14.5 us
    ppermute x4, starting transfers between devices, swap_parts(): return lax.ppermute(value, 'parts', [(i, i ^ 1) for i in range(count)])  14.4 us
    pallas_call x1, Pallas kernels, project_pair(): pl.pallas_call(functools.partial(pair_kernel, count=len(pieces), shard=sh...  12.1 us
  transfers between devices with their start and end apart: 19, of which 5 were waited for; matrix products, arithmetic and copies ran while one was open for 10% of the time, Pallas kernels for 4%

profile of v1, /device:TPU:34, one launch (start us, length us, event | category | flops | bytes accessed | tf_op | source)
XLA Modules:
  0.0 305.8 jit_solution(7985142701442711364)
XLA Ops:
  7.3 1.6 constant_dynamic-slice_fusion.4
  9.0 0.9 copy.42
  9.9 0.7 dynamic_slice.33
  10.7 4.2 %collective-permute-start = (bf16[256,1024]{1,0:T(8,128)(2,1)}, bf16[256,1024]{1,0:T(8,128)(2,1)S(1)}, u32[]{:S(2)}, u32[]{:S(2)}) collective-permute-start(bf16[256,1024]{1,0:T(8,128)(2,1)} %param.14), channel_id=1, source_target_pairs={{0,256},{256,0},{1,257},{257,1},{2,258},{258,2},{3,259},{259,3},{4... | collective-permute-start | bytes 1572872 | tf_op jit(solution)/shard_map/ppermute | solution.py:59
  14.9 2.0 collective-permute-start.13
  16.8 0.7 dynamic_slice.30
  17.6 1.3 dynamic_slice.37
  18.9 1.3 constant_dynamic-slice_fusion.1.refs_21_
  20.2 0.7 and_select_fusion.2
  20.8 0.7 fusion.21
  21.5 0.6 pad_add_fusion.at_ref
  22.3 0.1 iota_compare_fusion
  22.4 1.0 and_select_fusion
  23.5 80.0 %all_gather.6.refs_16_ = bf16[2048,128]{1,0:T(8,128)(2,1)S(1)} all-gather(bf16[256,128]{1,0:T(8,128)(2,1)S(1)} %dynamic-slice_bitcast_fusion), channel_id=1, replica_groups={{0,32,64,96,128,160,192,224},{8,40,72,104,136,168,200,232},{16,48,80,11..., dimensions={0}, use_global_device_ids=true | all-gather | bytes 589824 | tf_op jit(solution)/shard_map/all_gather | solution.py:103
  103.7 4.0 %collective-permute-start.2 = (bf16[528,1024]{1,0:T(8,128)(2,1)S(1)}, bf16[528,1024]{1,0:T(8,128)(2,1)}, u32[]{:S(2)}, u32[]{:S(2)}) collective-permute-start(bf16[528,1024]{1,0:T(8,128)(2,1)S(1)} %pad_maximum_fusion.refs_0_.refs_8_), channel_id=1, source_target_pairs={{0,2},{1,3},{2,4},{3,5},{4,6},{5,7},{6,0},{7,1},{8,10},{9,11},{10,... | collective-permute-start | bytes 3244040 | tf_op jit(solution)/shard_map/ppermute | solution.py:69
  107.6 2.0 collective-permute-start.4
  109.8 0.9 convert_reduce_fusion
  110.7 0.2 select_reduce_fusion
  111.1 1.3 gather_fusion.3
  112.8 1.4 gather_fusion
  114.2 17.5 %all-to-all-start = ((bf16[32,3,2,8,128]{4,3,2,1,0:T(8,128)(2,1)}), bf16[32,3,2,8,128]{4,3,2,1,0:T(8,128)(2,1)}, u32[]{:S(2)}, u32[]{:S(2)}) async-start(bf16[32,3,2,8,128]{4,3,2,1,0:T(8,128)(2,1)} %bitcast.95), calls=%async_computation | async-start | bytes 786432 | tf_op jit(solution)/shard_map/all_to_all | solution.py:265
  131.8 1.1 slice.65
  132.9 4.0 %collective-permute-start.6 = (bf16[256,1024]{1,0:T(8,128)(2,1)S(1)}, bf16[256,1024]{1,0:T(8,128)(2,1)S(1)}, u32[]{:S(2)}, u32[]{:S(2)}) collective-permute-start(bf16[256,1024]{1,0:T(8,128)(2,1)S(1)} %slice.65), channel_id=1, source_target_pairs={{0,2},{1,3},{2,4},{3,5},{4,6},{5,7},{6,0},{7,1},{8,10},{9,11},{10,... | collective-permute-start | bytes 1572872 | tf_op jit(solution)/shard_map/ppermute | solution.py:69
  136.9 2.0 collective-permute-start.7
  138.9 1.9 multiply_cosine_fusion
  140.8 1.9 collective-permute-start.1
  142.8 4.1 %collective-permute-start.11 = (bf16[1024,128]{1,0:T(8,128)(2,1)S(1)}, bf16[1024,128]{1,0:T(8,128)(2,1)S(1)}, u32[]{:S(2)}, u32[]{:S(2)}) collective-permute-start(bf16[1024,128]{1,0:T(8,128)(2,1)S(1)} %get-tuple-element.35), channel_id=1, source_target_pairs={{0,16},{8,24},{16,32},{24,40},{32,48},{40,56},{48,64},{56,72},{64,... | collective-permute-start | bytes 786440 | tf_op jit(solution)/shard_map/ppermute | solution.py:97
  146.9 3.9 %collective-permute-start.12 = (bf16[1024,128]{1,0:T(8,128)(2,1)S(1)}, bf16[1024,128]{1,0:T(8,128)(2,1)S(1)}, u32[]{:S(2)}, u32[]{:S(2)}) collective-permute-start(bf16[1024,128]{1,0:T(8,128)(2,1)S(1)} %get-tuple-element.34), channel_id=1, source_target_pairs={{0,240},{8,248},{16,0},{24,8},{32,16},{40,24},{48,32},{56,40},{64,... | collective-permute-start | bytes 786440 | tf_op jit(solution)/shard_map/ppermute | solution.py:97
  150.8 0.7 fusion.26
  151.6 3.2 %collective-permute-start.10 = (bf16[2048,128]{1,0:T(8,128)(2,1)S(1)}, bf16[2048,128]{1,0:T(8,128)(2,1)S(1)}, u32[]{:S(2)}, u32[]{:S(2)}) collective-permute-start(bf16[2048,128]{1,0:T(8,128)(2,1)S(1)} %all_gather.6.refs_16_), channel_id=1, source_target_pairs={{0,8},{8,16},{16,24},{24,32},{32,40},{40,48},{48,56},{56,64},{64,7... | collective-permute-start | bytes 1572872 | tf_op jit(solution)/shard_map/ppermute | solution.py:97
  154.8 0.8 constant_dynamic-update-slice_fusion.1
  155.6 1.9 collective-permute-start.3
  157.6 0.8 constant_dynamic-update-slice_fusion.refs_6_.refs_14_
  158.4 25.9 %collective-permute-done.11.refs_19_ = bf16[1024,128]{1,0:T(8,128)(2,1)S(1)} collective-permute-done((bf16[1024,128]{1,0:T(8,128)(2,1)S(1)}, bf16[1024,128]{1,0:T(8,128)(2,1)S(1)}, u32[]{:S(2)}, u32[]{:S(2)}) %collective-permute-start.11) | collective-permute-done | bytes 262176 | tf_op jit(solution)/shard_map/ppermute | solution.py:97
  184.4 1.9 collective-permute-start.5
  186.3 2.4 collective-permute-start.8
  188.8 0.2 convert_reduce_fusion.1
  189.0 11.7 %collective-permute-done.10.refs_18_ = bf16[2048,128]{1,0:T(8,128)(2,1)S(1)} collective-permute-done((bf16[2048,128]{1,0:T(8,128)(2,1)S(1)}, bf16[2048,128]{1,0:T(8,128)(2,1)S(1)}, u32[]{:S(2)}, u32[]{:S(2)}) %collective-permute-start.10) | collective-permute-done | bytes 524320 | tf_op jit(solution)/shard_map/ppermute | solution.py:97
  200.7 3.2 %collective-permute-start.9 = (bf16[2048,128]{1,0:T(8,128)(2,1)S(1)}, bf16[2048,128]{1,0:T(8,128)(2,1)}, u32[]{:S(2)}, u32[]{:S(2)}) collective-permute-start(bf16[2048,128]{1,0:T(8,128)(2,1)S(1)} %all_gather.6.refs_16_), channel_id=1, source_target_pairs={{0,248},{8,0},{16,8},{24,16},{32,24},{40,32},{48,40},{56,48},{64,5... | collective-permute-start | bytes 1572872 | tf_op jit(solution)/shard_map/ppermute | solution.py:97
  204.3 0.1 and_reduce_fusion
  204.5 11.9 %collective-permute-done.9.refs_17_ = bf16[2048,128]{1,0:T(8,128)(2,1)} collective-permute-done((bf16[2048,128]{1,0:T(8,128)(2,1)S(1)}, bf16[2048,128]{1,0:T(8,128)(2,1)}, u32[]{:S(2)}, u32[]{:S(2)}) %collective-permute-start.9) | collective-permute-done | bytes 524320 | tf_op jit(solution)/shard_map/ppermute | solution.py:97
  216.5 12.1 %shard_map.149 = (bf16[512,8192]{1,0:T(8,128)(2,1)}, bf16[512,128]{1,0:T(8,128)(2,1)}) custom-call(s32[13]{0:T(128)} %pad_add_fusion.at_ref, bf16[528,1024]{1,0:T(8,128)(2,1)} %copy-done.1, bf16[528,1024]{1,0:T(8,128)(2,1)} %collective-permute-done.1.refs_1_.refs_9_, bf16[528,1024]{1,0:T(8,128)(2,1)} %collective-permute-done.2.refs_2_.refs_10_, ...), custom_call_target="tpu_custom_call" | custom-call | tf_op jit(solution)/shard_map/pallas_call | solution.py:169
  228.6 0.9 fusion.33
  229.5 4.3 %collective-permute-start.14 = (bf16[2,128,1,128]{3,1,0,2:T(8,128)(2,1)S(1)}, bf16[2,128,1,128]{3,1,0,2:T(8,128)(2,1)S(1)}, u32[]{:S(2)}, u32[]{:S(2)}) collective-permute-start(bf16[2,128,1,128]{3,1,0,2:T(8,128)(2,1)S(1)} %bitcast.107), channel_id=1, source_target_pairs={{0,256},{256,0},{1,257},{257,1},{2,258},{258,2},{3,259},{259,3},{4... | collective-permute-start | bytes 196616 | tf_op jit(solution)/shard_map/ppermute | solution.py:59
  233.9 2.2 collective-permute-done.14
  236.2 0.7 gather_fusion.2
  236.9 0.8 broadcast_select_fusion
  237.7 18.5 %all-to-all-start.1 = ((bf16[32,2,2,8,128]{4,3,2,1,0:T(8,128)(2,1)}), bf16[32,2,2,8,128]{4,3,2,1,0:T(8,128)(2,1)S(1)}, u32[]{:S(2)}, u32[]{:S(2)}) async-start(bf16[32,2,2,8,128]{4,3,2,1,0:T(8,128)(2,1)} %broadcast_select_fusion), calls=%async_computation.1 | async-start | bytes 524288 | tf_op jit(solution)/shard_map/all_to_all | solution.py:304
  256.2 0.1 copy.49
  256.4 1.6 gather_fusion.1
  258.0 6.9 %convolution_add_fusion = f32[512,256]{0,1:T(8,128)S(1)} fusion(bf16[512,8192]{1,0:T(8,128)(2,1)} %get-tuple-element.23, bf16[8192,256]{1,0:T(8,128)(2,1)} %all-gather.2.cloned.1.call-done, f32[256]{0:T(256)S(1)} %copy-done.12), kind=kOutput, calls=%fused_computation.9 | convolution fusion | flops 2147614720 | bytes 13108224 | tf_op jit(solution)/shard_map/dot_general | solution.py:306
  265.1 0.2 copy.65
  265.3 0.2 copy.66
  265.5 0.5 copy-done.4
  266.0 0.1 subtract_convert_fusion
  266.1 0.1 fusion.13
  266.3 3.9 %collective-permute-start.15 = (bf16[2,128,2,128]{3,1,2,0:T(8,128)(2,1)S(1)}, bf16[2,128,2,128]{3,1,2,0:T(8,128)(2,1)S(1)}, u32[]{:S(2)}, u32[]{:S(2)}) collective-permute-start(bf16[2,128,2,128]{3,1,2,0:T(8,128)(2,1)S(1)} %copy.53), channel_id=1, source_target_pairs={{0,256},{256,0},{1,257},{257,1},{2,258},{258,2},{3,259},{259,3},{4... | collective-permute-start | bytes 393224 | tf_op jit(solution)/shard_map/ppermute | solution.py:59
  270.4 25.6 %all-to-all-done.1 = bf16[32,2,2,8,128]{4,3,2,1,0:T(8,128)(2,1)S(1)} async-done(((bf16[32,2,2,8,128]{4,3,2,1,0:T(8,128)(2,1)}), bf16[32,2,2,8,128]{4,3,2,1,0:T(8,128)(2,1)S(1)}, u32[]{:S(2)}, u32[]{:S(2)}) %all-to-all-start.1) | async-done | bytes 262176 | tf_op jit(solution)/shard_map/all_to_all | solution.py:304
  296.1 0.4 fusion.34
  296.5 0.3 fusion
  296.8 0.5 fusion.3
  297.3 0.2 copy.57
  297.5 0.7 copy.71
  298.2 0.7 copy.74
  (88 shorter events, 2.4 us)
Async XLA Ops:
  7.2 105.6 %copy-start = (bf16[128,2,8,128]{3,2,1,0:T(8,128)(2,1)S(1)}, bf16[128,2,8,128]{3,2,1,0:T(8,128)(2,1)}, u32[]{:S(2)}) copy-start(bf16[128,2,8,128]{3,2,1,0:T(8,128)(2,1)} %param.20) | copy-start | bytes 1572868
  7.2 96.4 %copy-start.6 = (bf16[256,1024]{1,0:T(8,128)(2,1)S(1)}, bf16[256,1024]{1,0:T(8,128)(2,1)}, u32[]{:S(2)}) copy-start(bf16[256,1024]{1,0:T(8,128)(2,1)} %param.14) | copy-start | bytes 1572868
  7.2 96.4 %copy-start.11 = (bf16[1024]{0:T(1024)(128)(2,1)S(1)}, bf16[1024]{0:T(1024)(128)(2,1)}, u32[]{:S(2)}) copy-start(bf16[1024]{0:T(1024)(128)(2,1)} %param.15) | copy-start | bytes 6148
  7.2 250.8 %all-gather.2.cloned.1.call-start = ((), (), s32[]{:S(2)}) async-start(), calls=%async_computation.2 | async-start | bytes 4325376 | tf_op jit(solution)/shard_map/all_gather | solution.py:223
  10.7 98.9 %copy-start.10 = (s32[64,32]{0,1:T(8,128)S(1)}, s32[64,32]{0,1:T(8,128)}, u32[]{:S(2)}) copy-start(s32[64,32]{0,1:T(8,128)} %param.21) | copy-start | bytes 24580
  10.7 92.9 %collective-permute-start = (bf16[256,1024]{1,0:T(8,128)(2,1)}, bf16[256,1024]{1,0:T(8,128)(2,1)S(1)}, u32[]{:S(2)}, u32[]{:S(2)}) collective-permute-start(bf16[256,1024]{1,0:T(8,128)(2,1)} %param.14), channel_id=1, source_target_pairs={{0,256},{256,0},{1,257},{257,1},{2,258},{258,2},{3,259},{259,3},{4... | collective-permute-start | bytes 1572872 | tf_op jit(solution)/shard_map/ppermute | solution.py:59
  14.9 88.6 %collective-permute-start.13 = (s32[2]{0:T(128)S(1)}, s32[2]{0:T(128)S(1)}, u32[]{:S(2)}, u32[]{:S(2)}) collective-permute-start(s32[2]{0:T(128)S(1)} %dynamic_slice.33), channel_id=1, source_target_pairs={{0,256},{256,0},{1,257},{257,1},{2,258},{258,2},{3,259},{259,3},{4... | collective-permute-start | bytes 32 | tf_op jit(solution)/shard_map/ppermute | solution.py:59
  23.5 212.6 %copy-start.13 = (pred[2,128]{1,0:T(4,128)(4,1)}, pred[2,128]{1,0:T(4,128)(4,1)S(1)}, u32[]{:S(2)}) copy-start(pred[2,128]{1,0:T(4,128)(4,1)S(1)} %iota_compare_fusion.8) | copy-start | bytes 772
  103.5 97.2 %copy-start.3 = (bf16[2048,128]{1,0:T(8,128)(2,1)}, bf16[2048,128]{1,0:T(8,128)(2,1)S(1)}, u32[]{:S(2)}) copy-start(bf16[2048,128]{1,0:T(8,128)(2,1)S(1)} %all_gather.6.refs_16_) | copy-start | bytes 1572868
  103.7 37.1 %copy-start.1 = (bf16[528,1024]{1,0:T(8,128)(2,1)}, bf16[528,1024]{1,0:T(8,128)(2,1)S(1)}, u32[]{:S(2)}) copy-start(bf16[528,1024]{1,0:T(8,128)(2,1)S(1)} %pad_maximum_fusion.refs_0_.refs_8_) | copy-start | bytes 3244036
  103.7 28.2 %collective-permute-start.2 = (bf16[528,1024]{1,0:T(8,128)(2,1)S(1)}, bf16[528,1024]{1,0:T(8,128)(2,1)}, u32[]{:S(2)}, u32[]{:S(2)}) collective-permute-start(bf16[528,1024]{1,0:T(8,128)(2,1)S(1)} %pad_maximum_fusion.refs_0_.refs_8_), channel_id=1, source_target_pairs={{0,2},{1,3},{2,4},{3,5},{4,6},{5,7},{6,0},{7,1},{8,10},{9,11},{10,... | collective-permute-start | bytes 3244040 | tf_op jit(solution)/shard_map/ppermute | solution.py:69
  107.6 29.2 %collective-permute-start.4 = (bf16[528,1024]{1,0:T(8,128)(2,1)S(1)}, bf16[528,1024]{1,0:T(8,128)(2,1)S(1)}, u32[]{:S(2)}, u32[]{:S(2)}) collective-permute-start(bf16[528,1024]{1,0:T(8,128)(2,1)S(1)} %pad_maximum_fusion.refs_0_.refs_8_), channel_id=1, source_target_pairs={{0,6},{1,7},{2,0},{3,1},{4,2},{5,3},{6,4},{7,5},{8,14},{9,15},{10,... | collective-permute-start | bytes 3244040 | tf_op jit(solution)/shard_map/ppermute | solution.py:69
  114.2 123.5 %all-to-all-start = ((bf16[32,3,2,8,128]{4,3,2,1,0:T(8,128)(2,1)}), bf16[32,3,2,8,128]{4,3,2,1,0:T(8,128)(2,1)}, u32[]{:S(2)}, u32[]{:S(2)}) async-start(bf16[32,3,2,8,128]{4,3,2,1,0:T(8,128)(2,1)} %bitcast.95), calls=%async_computation | async-start | bytes 786432 | tf_op jit(solution)/shard_map/all_to_all | solution.py:265
  132.9 18.6 %collective-permute-start.6 = (bf16[256,1024]{1,0:T(8,128)(2,1)S(1)}, bf16[256,1024]{1,0:T(8,128)(2,1)S(1)}, u32[]{:S(2)}, u32[]{:S(2)}) collective-permute-start(bf16[256,1024]{1,0:T(8,128)(2,1)S(1)} %slice.65), channel_id=1, source_target_pairs={{0,2},{1,3},{2,4},{3,5},{4,6},{5,7},{6,0},{7,1},{8,10},{9,11},{10,... | collective-permute-start | bytes 1572872 | tf_op jit(solution)/shard_map/ppermute | solution.py:69
  136.9 47.5 %copy-start.2 = (bf16[528,1024]{1,0:T(8,128)(2,1)}, bf16[528,1024]{1,0:T(8,128)(2,1)S(1)}, u32[]{:S(2)}) copy-start(bf16[528,1024]{1,0:T(8,128)(2,1)S(1)} %collective-permute-done.4.refs_4_.refs_12_) | copy-start | bytes 3244036
  136.9 18.7 %collective-permute-start.7 = (bf16[272,1024]{1,0:T(8,128)(2,1)S(1)}, bf16[272,1024]{1,0:T(8,128)(2,1)S(1)}, u32[]{:S(2)}, u32[]{:S(2)}) collective-permute-start(bf16[272,1024]{1,0:T(8,128)(2,1)S(1)} %slice.66), channel_id=1, source_target_pairs={{0,6},{1,7},{2,0},{3,1},{4,2},{5,3},{6,4},{7,5},{8,14},{9,15},{10,... | collective-permute-start | bytes 1671176 | tf_op jit(solution)/shard_map/ppermute | solution.py:69
  140.8 75.7 %collective-permute-start.1 = (bf16[528,1024]{1,0:T(8,128)(2,1)S(1)}, bf16[528,1024]{1,0:T(8,128)(2,1)}, u32[]{:S(2)}, u32[]{:S(2)}) collective-permute-start(bf16[528,1024]{1,0:T(8,128)(2,1)S(1)} %pad_maximum_fusion.refs_0_.refs_8_), channel_id=1, source_target_pairs={{0,1},{1,0},{2,3},{3,2},{4,5},{5,4},{6,7},{7,6},{8,9},{9,8},{10,11... | collective-permute-start | bytes 3244040 | tf_op jit(solution)/shard_map/ppermute | solution.py:64
  142.8 41.6 %collective-permute-start.11 = (bf16[1024,128]{1,0:T(8,128)(2,1)S(1)}, bf16[1024,128]{1,0:T(8,128)(2,1)S(1)}, u32[]{:S(2)}, u32[]{:S(2)}) collective-permute-start(bf16[1024,128]{1,0:T(8,128)(2,1)S(1)} %get-tuple-element.35), channel_id=1, source_target_pairs={{0,16},{8,24},{16,32},{24,40},{32,48},{40,56},{48,64},{56,72},{64,... | collective-permute-start | bytes 786440 | tf_op jit(solution)/shard_map/ppermute | solution.py:97
  146.9 39.4 %collective-permute-start.12 = (bf16[1024,128]{1,0:T(8,128)(2,1)S(1)}, bf16[1024,128]{1,0:T(8,128)(2,1)S(1)}, u32[]{:S(2)}, u32[]{:S(2)}) collective-permute-start(bf16[1024,128]{1,0:T(8,128)(2,1)S(1)} %get-tuple-element.34), channel_id=1, source_target_pairs={{0,240},{8,248},{16,0},{24,8},{32,16},{40,24},{48,32},{56,40},{64,... | collective-permute-start | bytes 786440 | tf_op jit(solution)/shard_map/ppermute | solution.py:97
  151.6 49.2 %collective-permute-start.10 = (bf16[2048,128]{1,0:T(8,128)(2,1)S(1)}, bf16[2048,128]{1,0:T(8,128)(2,1)S(1)}, u32[]{:S(2)}, u32[]{:S(2)}) collective-permute-start(bf16[2048,128]{1,0:T(8,128)(2,1)S(1)} %all_gather.6.refs_16_), channel_id=1, source_target_pairs={{0,8},{8,16},{16,24},{24,32},{32,40},{40,48},{48,56},{56,64},{64,7... | collective-permute-start | bytes 1572872 | tf_op jit(solution)/shard_map/ppermute | solution.py:97
  155.6 60.8 %collective-permute-start.3 = (bf16[528,1024]{1,0:T(8,128)(2,1)}, bf16[528,1024]{1,0:T(8,128)(2,1)}, u32[]{:S(2)}, u32[]{:S(2)}) collective-permute-start(bf16[528,1024]{1,0:T(8,128)(2,1)} %collective-permute-done.2.refs_2_.refs_10_), channel_id=1, source_target_pairs={{0,1},{1,0},{2,3},{3,2},{4,5},{5,4},{6,7},{7,6},{8,9},{9,8},{10,11... | collective-permute-start | bytes 3244040 | tf_op jit(solution)/shard_map/ppermute | solution.py:64
  184.4 19.7 %copy-start.8 = (bf16[1024,128]{1,0:T(8,128)(2,1)}, bf16[1024,128]{1,0:T(8,128)(2,1)S(1)}, u32[]{:S(2)}) copy-start(bf16[1024,128]{1,0:T(8,128)(2,1)S(1)} %collective-permute-done.11.refs_19_) | copy-start | bytes 786436
  184.4 32.1 %collective-permute-start.5 = (bf16[528,1024]{1,0:T(8,128)(2,1)S(1)}, bf16[528,1024]{1,0:T(8,128)(2,1)}, u32[]{:S(2)}, u32[]{:S(2)}) collective-permute-start(bf16[528,1024]{1,0:T(8,128)(2,1)S(1)} %collective-permute-done.4.refs_4_.refs_12_), channel_id=1, source_target_pairs={{0,1},{1,0},{2,3},{3,2},{4,5},{5,4},{6,7},{7,6},{8,9},{9,8},{10,11... | collective-permute-start | bytes 3244040 | tf_op jit(solution)/shard_map/ppermute | solution.py:64
  186.3 17.8 %copy-start.9 = (bf16[1024,128]{1,0:T(8,128)(2,1)}, bf16[1024,128]{1,0:T(8,128)(2,1)S(1)}, u32[]{:S(2)}) copy-start(bf16[1024,128]{1,0:T(8,128)(2,1)S(1)} %collective-permute-done.12.refs_20_) | copy-start | bytes 786436
  186.3 30.1 %collective-permute-start.8 = (bf16[528,1024]{1,0:T(8,128)(2,1)}, bf16[528,1024]{1,0:T(8,128)(2,1)}, u32[]{:S(2)}, u32[]{:S(2)}) collective-permute-start(bf16[528,1024]{1,0:T(8,128)(2,1)} %constant_dynamic-update-slice_fusion.refs_6_.refs_14_), channel_id=1, source_target_pairs={{0,1},{1,0},{2,3},{3,2},{4,5},{5,4},{6,7},{7,6},{8,9},{9,8},{10,11... | collective-permute-start | bytes 3244040 | tf_op jit(solution)/shard_map/ppermute | solution.py:64
  200.7 3.2 %copy-start.5 = (bf16[2048,128]{1,0:T(8,128)(2,1)}, bf16[2048,128]{1,0:T(8,128)(2,1)S(1)}, u32[]{:S(2)}) copy-start(bf16[2048,128]{1,0:T(8,128)(2,1)S(1)} %collective-permute-done.10.refs_18_) | copy-start | bytes 1572868
  200.7 15.7 %collective-permute-start.9 = (bf16[2048,128]{1,0:T(8,128)(2,1)S(1)}, bf16[2048,128]{1,0:T(8,128)(2,1)}, u32[]{:S(2)}, u32[]{:S(2)}) collective-permute-start(bf16[2048,128]{1,0:T(8,128)(2,1)S(1)} %all_gather.6.refs_16_), channel_id=1, source_target_pairs={{0,248},{8,0},{16,8},{24,16},{32,24},{40,32},{48,40},{56,48},{64,5... | collective-permute-start | bytes 1572872 | tf_op jit(solution)/shard_map/ppermute | solution.py:97
  228.6 29.4 %copy-start.12 = (f32[256]{0:T(256)S(1)}, f32[256]{0:T(256)}, u32[]{:S(2)}) copy-start(f32[256]{0:T(256)} %dynamic_slice.37) | copy-start | bytes 3076
  229.5 6.5 %collective-permute-start.14 = (bf16[2,128,1,128]{3,1,0,2:T(8,128)(2,1)S(1)}, bf16[2,128,1,128]{3,1,0,2:T(8,128)(2,1)S(1)}, u32[]{:S(2)}, u32[]{:S(2)}) collective-permute-start(bf16[2,128,1,128]{3,1,0,2:T(8,128)(2,1)S(1)} %bitcast.107), channel_id=1, source_target_pairs={{0,256},{256,0},{1,257},{257,1},{2,258},{258,2},{3,259},{259,3},{4... | collective-permute-start | bytes 196616 | tf_op jit(solution)/shard_map/ppermute | solution.py:59
  237.7 58.3 %all-to-all-start.1 = ((bf16[32,2,2,8,128]{4,3,2,1,0:T(8,128)(2,1)}), bf16[32,2,2,8,128]{4,3,2,1,0:T(8,128)(2,1)S(1)}, u32[]{:S(2)}, u32[]{:S(2)}) async-start(bf16[32,2,2,8,128]{4,3,2,1,0:T(8,128)(2,1)} %broadcast_select_fusion), calls=%async_computation.1 | async-start | bytes 524288 | tf_op jit(solution)/shard_map/all_to_all | solution.py:304
  265.0 1.0 copy-start.4
  266.1 30.0 %copy-start.7 = (pred[2,128,384]{1,2,0:T(8,128)(4,1)S(1)}, pred[2,128,384]{1,2,0:T(8,128)(4,1)}, u32[]{:S(2)}) copy-start(pred[2,128,384]{1,2,0:T(8,128)(4,1)} %and_select_fusion) | copy-start | bytes 294916
  266.3 29.7 %collective-permute-start.15 = (bf16[2,128,2,128]{3,1,2,0:T(8,128)(2,1)S(1)}, bf16[2,128,2,128]{3,1,2,0:T(8,128)(2,1)S(1)}, u32[]{:S(2)}, u32[]{:S(2)}) collective-permute-start(bf16[2,128,2,128]{3,1,2,0:T(8,128)(2,1)S(1)} %copy.53), channel_id=1, source_target_pairs={{0,256},{256,0},{1,257},{257,1},{2,258},{258,2},{3,259},{259,3},{4... | collective-permute-start | bytes 393224 | tf_op jit(solution)/shard_map/ppermute | solution.py:59
  296.1 0.7 copy-start.14
Sparse Core Ops, SparseCore 0:
  10.1 204.6 all-gather.1
